TPU v7x, 256 devices: a whole 4x4x8 slice. The times are simulated.
256 devices in a mesh: wave: 32 (over z, x_hi, core), lev: 8 (over y, x_lo).
Axes of the slice: x: 4 (x_hi: 2, x_lo: 2; x = x_hi * 2 + x_lo), y: 4, z: 8, core: 2. Of those that a mesh axis runs over, the one named last changes fastest.
Arguments:
- spectral: float32 [136, 1024, 2562], P('lev', 'wave'), may hold values from -6 to 6
- to_modes: float32 [136, 136], replicated, may hold values from -3 to 3
- from_modes: float32 [136, 136], replicated, may hold values from -3 to 3
- depth: float32 [136], replicated, may hold values from 0.02 to 50
- owner: int32 [512], replicated, may hold values from 0 to 31, as said below
Outputs:
- solved: float32 [136, 512, 2562], P('lev', 'wave')
Inputs may be any that keep to these rules, and one draw needn't show every extreme that they name: `owner`: group q holds the pairs q * 1 to q * 1 + 1 - 1; a device stores its groups in increasing q from its first slot on, 1 slots each, and leaves its other slots unused. The 16 groups with the same q // 16 have 16 different owners. A device owns at most 32 groups, and some device exactly that many.
All inputs are finite; a program needn't handle non-finite values.
Results may differ from a plain program's by a relative error of at most 0.000075.
Values sent between devices are 32-bit elements; how exact they have to be, the bound alone decides.
A program may use at most 128 MiB of HBM per device.

v0:
```python
import jax
import jax.numpy as jnp
from jax import lax
from jax.sharding import PartitionSpec as P

NT = 1279
KPAIR = 1


def split_up(shard, dim, peers):
    before, after = (shard.shape[:dim], shard.shape[dim + 1 :])
    return jnp.moveaxis(shard.reshape(*before, peers, -1, *after), dim, 0)


def cut_rows(length, count):
    unit = 8 if length >= 8 * count else 1
    return [length // unit * k // count * unit for k in range(1, count)]


def joined_along(parts, dim):
    parts = jnp.moveaxis(parts, 0, dim)
    lengths = parts.shape
    return parts.reshape(*lengths[:dim], lengths[dim] * lengths[dim + 1], *lengths[dim + 2 :])


def exchange_in_pieces(shard, axis, pieces, split_dim, concat_dim):
    parts = split_up(shard, split_dim, lax.axis_size(axis))
    split_at = max(range(1, max(2, parts.ndim - 1)), key=lambda d: parts.shape[d])
    done = []
    for share in jnp.split(parts, cut_rows(parts.shape[split_at], pieces), axis=split_at):
        if share.size:
            done.append(lax.all_to_all(share, axis, split_axis=0, concat_axis=0, tiled=True))
    return joined_along(jnp.concatenate(done, axis=split_at), concat_dim)


def degree_ratio(pairs_here, columns, width):
    slot_index = columns // width
    within = columns % width % (NT + 2)
    match = slot_index[None, :] == jnp.arange(pairs_here.shape[0], dtype=jnp.int32)[:, None]
    pair = jnp.sum(jnp.where(match, pairs_here[:, None], 0), axis=0)
    degree = jnp.where(within <= NT - pair, pair + within, within - 1)
    return (degree * (degree + 1)).astype(jnp.float32) / float(NT * (NT + 1))


def per_device(spectral, to_modes, from_modes, depth, owner):
    waves = lax.axis_size("wave")
    groups = waves // 2
    own_index = lax.axis_index("wave")
    numbers = jnp.arange(groups * waves, dtype=jnp.int32)
    same = owner[:, None] == owner[None, :]
    rank = jnp.sum((same & (numbers[None, :] < numbers[:, None])).astype(jnp.int32), axis=1)
    mine = owner == own_index
    pairs_target = own_index * groups * KPAIR + jnp.arange(groups * KPAIR, dtype=jnp.int32)
    offsets = jnp.arange(KPAIR, dtype=jnp.int32)
    mine_grid = mine.reshape(waves, groups)
    rank_grid = rank.reshape(waves, groups)
    first_slot = jnp.sum(jnp.where(mine_grid, rank_grid, 0), axis=1) * KPAIR
    picks = (first_slot[:, None] + offsets[None, :]).reshape(waves * KPAIR)
    outgoing = jnp.take(spectral, picks, axis=1)
    incoming = exchange_in_pieces(outgoing, "wave", 2, 1, 1)
    senders = lax.dynamic_slice_in_dim(owner, own_index * groups, groups)
    places = (senders[:, None] * KPAIR + offsets[None, :]).reshape(groups * KPAIR)
    balanced = jnp.take(incoming, places, axis=1)
    level_rows, number, width = balanced.shape
    flat = balanced.reshape(level_rows, number * width)
    lev_index = lax.axis_index("lev")
    columns = lax.all_to_all(flat, "lev", split_axis=1, concat_axis=0, tiled=True)
    share = columns.shape[1]
    placed = lev_index * share + jnp.arange(share, dtype=jnp.int32)
    ratio = degree_ratio(pairs_target, placed, width)
    modes = jnp.dot(
        to_modes, columns, precision=lax.Precision.HIGHEST, preferred_element_type=jnp.float32
    )
    scaled = modes / (1.0 + depth[:, None] * ratio[None, :])
    mixed = jnp.dot(
        from_modes, scaled, precision=lax.Precision.HIGHEST, preferred_element_type=jnp.float32
    )
    result = lax.all_to_all(mixed, "lev", split_axis=0, concat_axis=1, tiled=True)
    return result.reshape(level_rows, number, width)


def solution(mesh):
    placed = (P("lev", "wave", None), P(), P(), P(), P())
    return jax.shard_map(
        per_device, mesh=mesh, in_specs=placed, out_specs=P("lev", "wave", None), check_vma=False
    )
```

profile of v0, /device:TPU:3, one launch (start us, length us, event | category | flops | bytes accessed | tf_op | source)
XLA Modules:
  0.0 315.5 jit_solution(13889433469654502738)
XLA Ops:
  0.0 0.0 copy-start
  0.0 1.0 convert_reduce_fusion
  1.0 0.7 compare_select_fusion.3
  1.7 0.1 select_n.90
  1.8 0.1 reduce_sum.30
  1.9 11.3 %gather_fusion = f32[32,17,2562]{2,0,1:T(8,128)} fusion(f32[17,32,2562]{2,1,0:T(8,128)} %param.5, s32[1024]{0:T(1024)S(1)} %pad_clamp_fusion.1), kind=kCustom, calls=%fused_computation | custom fusion | bytes 11149952 | tf_op jit(solution)/shard_map/jit(_take)/gather | solution.py:59
  13.2 3.3 %fusion.1 = f32[32,17,1,2562]{3,0,1,2:T(8,128)S(1)} fusion(f32[32,17,2562]{2,0,1:T(8,128)} %gather_fusion, pred[32]{0:T(512)(128)(4,1)S(1)} %compare_and_fusion), kind=kLoop, calls=%fused_computation.7 | loop fusion | flops 1393728 | bytes 11149856 | tf_op jit(solution)/shard_map/transpose | solution.py:12
  16.5 0.0 copy-start.1
  16.5 2.5 copy-done.1
  19.0 0.2 split.9
  19.3 4.9 %copy.27 = f32[32,9,1,2562]{3,2,1,0:T(1,128)} copy(f32[32,9,1,2562]{3,0,1,2:T(8,128)S(1)} %split.9) | data formatting | bytes 5902848 | tf_op jit(solution)/shard_map/split | solution.py:30
  24.1 11.5 %all-to-all-start.1 = ((f32[32,9,1,2562]{3,2,1,0:T(1,128)}), f32[32,9,1,2562]{3,2,1,0:T(1,128)S(1)}, u32[]{:S(2)}, u32[]{:S(2)}) async-start(f32[32,9,1,2562]{3,2,1,0:T(1,128)} %copy.27), calls=%async_computation.1 | async-start | bytes 6193152 | tf_op jit(solution)/shard_map/all_to_all | solution.py:32
  35.7 0.0 slice-start
  35.7 1.8 slice-done
  37.4 3.1 copy.26
  40.6 65.9 %all-to-all-done.1 = f32[32,9,1,2562]{3,2,1,0:T(1,128)S(1)} async-done(((f32[32,9,1,2562]{3,2,1,0:T(1,128)}), f32[32,9,1,2562]{3,2,1,0:T(1,128)S(1)}, u32[]{:S(2)}, u32[]{:S(2)}) %all-to-all-start.1) | async-done | bytes 2951456 | tf_op jit(solution)/shard_map/all_to_all | solution.py:32
  106.5 7.1 %all-to-all-start = ((f32[32,8,1,2562]{3,1,2,0:T(8,128)}), f32[32,8,1,2562]{3,1,2,0:T(8,128)}, u32[]{:S(2)}, u32[]{:S(2)}) async-start(f32[32,8,1,2562]{3,1,2,0:T(8,128)} %copy.26), calls=%async_computation | async-start | bytes 5505024 | tf_op jit(solution)/shard_map/all_to_all | solution.py:32
  113.6 0.8 compare_and_fusion.1
  114.4 0.1 broadcast_in_dim.53
  114.4 0.1 broadcast_in_dim.54
  114.6 0.1 broadcast_in_dim.55
  114.7 2.9 copy.29
  117.7 59.5 %all-to-all-done = f32[32,8,1,2562]{3,1,2,0:T(8,128)} async-done(((f32[32,8,1,2562]{3,1,2,0:T(8,128)}), f32[32,8,1,2562]{3,1,2,0:T(8,128)}, u32[]{:S(2)}, u32[]{:S(2)}) %all-to-all-start) | async-done | bytes 2623520 | tf_op jit(solution)/shard_map/all_to_all | solution.py:32
  177.2 7.1 %maximum_bitcast_fusion = f32[17,32,2562]{2,0,1:T(8,128)} fusion(f32[32,9,1,2562]{3,1,0,2:T(8,128)} %copy.29, f32[32,8,1,2562]{3,1,0,2:T(8,128)} %bitcast.5), kind=kLoop, calls=%fused_computation.2 | loop fusion | flops 1393728 | bytes 11149824 | tf_op jit(solution)/shard_map/reshape | solution.py:23
  184.3 6.1 %gather_fusion.1 = f32[16,17,2562]{2,1,0:T(8,128)} fusion(f32[17,32,2562]{2,0,1:T(8,128)} %maximum_bitcast_fusion, s32[1024]{0:T(1024)S(1)} %pad_clamp_fusion), kind=kCustom, calls=%fused_computation.1 | custom fusion | bytes 5574976 | tf_op jit(solution)/shard_map/jit(_take)/gather | solution.py:63
  190.5 2.7 copy.30
  193.2 2.3 gather.15
  195.4 2.0 broadcast_select_fusion
  197.5 2.5 copy.31
  200.0 5.6 %all-to-all-start.2 = ((f32[17,8,5124]{2,0,1:T(8,128)}), f32[17,8,5124]{2,0,1:T(8,128)}, u32[]{:S(2)}, u32[]{:S(2)}) async-start(f32[17,8,5124]{2,0,1:T(8,128)} %copy.31), calls=%async_computation.2 | async-start | bytes 8060928 | tf_op jit(solution)/shard_map/all_to_all | solution.py:67
  205.6 0.1 select_reduce_fusion
  205.8 46.2 %all-to-all-done.2 = f32[17,8,5124]{2,0,1:T(8,128)} async-done(((f32[17,8,5124]{2,0,1:T(8,128)}), f32[17,8,5124]{2,0,1:T(8,128)}, u32[]{:S(2)}, u32[]{:S(2)}) %all-to-all-start.2) | async-done | bytes 2787488 | tf_op jit(solution)/shard_map/all_to_all | solution.py:67
  252.0 0.0 copy-start.3
  252.0 2.5 all_to_all.34
  254.5 0.0 copy-done
  254.5 0.0 copy-done.3
  254.5 0.0 copy-start.2
  254.5 3.1 fusion
  257.7 0.0 copy-done.2
  257.7 2.9 convolution_bitcast_fusion
  260.6 2.3 all_to_all.35
  262.9 49.7 %all_to_all.42 = f32[8,17,5124]{2,1,0:T(8,128)S(1)} all-to-all(f32[8,17,5124]{2,1,0:T(8,128)} %all_to_all.35), channel_id=1, replica_groups=mesh['wave'=32,'lev'=8] {'lev'}, dimensions={0} | all-to-all | bytes 5574912 | tf_op jit(solution)/shard_map/all_to_all | solution.py:78
  312.6 0.5 copy.32
  313.1 2.3 reshape.102
  (7 shorter events, 0.1 us)
Async XLA Ops:
  0.0 254.5 %copy-start = (f32[136,136]{1,0:T(8,128)S(1)}, f32[136,136]{1,0:T(8,128)}, u32[]{:S(2)}) copy-start(f32[136,136]{1,0:T(8,128)} %param.6) | copy-start | bytes 221956
  16.5 2.5 copy-start.1
  24.1 82.4 %all-to-all-start.1 = ((f32[32,9,1,2562]{3,2,1,0:T(1,128)}), f32[32,9,1,2562]{3,2,1,0:T(1,128)S(1)}, u32[]{:S(2)}, u32[]{:S(2)}) async-start(f32[32,9,1,2562]{3,2,1,0:T(1,128)} %copy.27), calls=%async_computation.1 | async-start | bytes 6193152 | tf_op jit(solution)/shard_map/all_to_all | solution.py:32
  35.7 1.8 slice-start
  106.5 70.7 %all-to-all-start = ((f32[32,8,1,2562]{3,1,2,0:T(8,128)}), f32[32,8,1,2562]{3,1,2,0:T(8,128)}, u32[]{:S(2)}, u32[]{:S(2)}) async-start(f32[32,8,1,2562]{3,1,2,0:T(8,128)} %copy.26), calls=%async_computation | async-start | bytes 5505024 | tf_op jit(solution)/shard_map/all_to_all | solution.py:32
  200.0 52.0 %all-to-all-start.2 = ((f32[17,8,5124]{2,0,1:T(8,128)}), f32[17,8,5124]{2,0,1:T(8,128)}, u32[]{:S(2)}, u32[]{:S(2)}) async-start(f32[17,8,5124]{2,0,1:T(8,128)} %copy.31), calls=%async_computation.2 | async-start | bytes 8060928 | tf_op jit(solution)/shard_map/all_to_all | solution.py:67
  252.0 2.5 copy-start.3
  254.5 3.2 copy-start.2
where the time goes:
time: 320 us; the launch traced here: 315 us
  waiting for transfers between devices  172 us (54%)
  blocking collectives  49.7 us (16%)
  local copies, waits for them, and re-layouts  48.4 us (15%)
  starting transfers between devices  24.2 us (8%)
  other arithmetic  15.3 us (5%)
  matrix products  6.02 us (2%)
    all_to_all x2, waiting for transfers between devices, exchange_in_pieces(): lax.all_to_all(share, axis, split_axis=0, concat_axis=0, tiled=True)  125 us
    all_to_all x1, blocking collectives, per_device(): lax.all_to_all(mixed, 'lev', split_axis=0, concat_axis=1, tiled=True)  49.7 us
    all_to_all x1, waiting for transfers between devices, per_device(): lax.all_to_all(flat, 'lev', split_axis=1, concat_axis=0, tiled=True)  46.2 us
    all_to_all x2, starting transfers between devices, exchange_in_pieces(): lax.all_to_all(share, axis, split_axis=0, concat_axis=0, tiled=True)  18.6 us
    gather x1, local copies, waits for them, and re-layouts, per_device(): outgoing = jnp.take(spectral, picks, axis=1)  11.3 us
    gather x3, local copies, waits for them, and re-layouts, per_device(): balanced = jnp.take(incoming, places, axis=1)  11.1 us
    split x5, local copies, waits for them, and re-layouts, exchange_in_pieces(): jnp.split(parts, cut_rows(parts.shape[split_at], pieces), axis=split_at)  9.99 us
    reshape x1, other arithmetic, joined_along(): parts.reshape(*lengths[:dim], lengths[dim] * lengths[dim + 1], *lengths[d...  7.13 us
  transfers between devices with their start and end apart: 3, of which 3 were waited for; matrix products, arithmetic and copies ran while one was open for 2% of the time, Pallas kernels for 0%

commit v1 on v0

v1 whole, which is shorter than its diff:
```python
import functools

import jax
import jax.numpy as jnp
from jax import lax
from jax.experimental import pallas as pl
from jax.experimental.pallas import tpu as pltpu
from jax.sharding import PartitionSpec as P

NT = 1279
PLEN = NT + 2
LANES = 128
SIZES = (8, 8, 4)
MESH = pl.DeviceIdType.MESH


def rows_of(levels, tiles, rest):
    return -(-(levels * tiles + (rest > 0)) // 8) * 8


def kernel(
    waves, levs, number, levels, slots, rest, chunks,
    picks, senders, spectral, edge, to_modes, from_modes, depth, out, edge_out,
    held, result, matrix, packs, lands, picked, blocks, backs, homes,
    in_sem, out_sem, send1, recv1, send2, recv2, send3, recv3,
):
    me = lax.axis_index("wave")
    lev = lax.axis_index("lev")
    per = number // levs
    n = len(chunks)
    last = n - 1

    def load(c, t):
        at = chunks[c][0] + t
        return pltpu.make_async_copy(
            spectral.at[:, pl.ds(at * LANES, LANES)], held[c].at[t], in_sem.at[at]
        )

    def store(c, t):
        at = chunks[c][0] + t
        return pltpu.make_async_copy(
            result.at[at], out.at[:, pl.ds(at * LANES, LANES)], out_sem.at[at]
        )

    def each_tile(c, act):
        for t in range(chunks[c][1]):
            act(c, t)

    def wave_copy(c, k, at=None):
        peer = lax.rem(me + k, waves)
        at = me if at is None else peer
        return pltpu.make_async_remote_copy(
            src_ref=packs[c].at[peer], dst_ref=lands[c].at[at],
            send_sem=send1.at[c, peer], recv_sem=recv1.at[c, at],
            device_id={"wave": peer}, device_id_type=MESH,
        )

    def place(ref, c, at):
        if len(ref.shape) > 2:
            return ref.at[at]
        size = per * chunks[c][2]
        return ref.at[pl.ds(pl.multiple_of(at * size, 8), size)]

    def lev_copy(source, target, send, recv, c, peer, at):
        return pltpu.make_async_remote_copy(
            src_ref=place(source[c], c, peer), dst_ref=place(target[c], c, at),
            send_sem=send.at[c, peer], recv_sem=recv.at[c, at],
            device_id={"lev": peer}, device_id_type=MESH,
        )

    def modal(c, peer, at):
        return lev_copy(picked, blocks, send2, recv2, c, peer, at)

    def back(c, peer, at):
        return lev_copy(backs, homes, send3, recv3, c, peer, at)

    def gather(c):
        tiles = chunks[c][1]

        @pl.loop(0, waves)
        def _(d):
            slot = picks[d]
            for t in range(tiles):
                packs[c][d, pl.ds(t, levels, stride=tiles), :] = held[c][
                    t, pl.ds(slot, levels, stride=slots), :
                ]
            if c == last and rest:
                packs[c][d, pl.ds(levels * tiles, 1), :] = edge[pl.ds(slot, 1), :]

    def each_wave(act):
        pl.loop(1, waves)(act)

    def each_lev(act):
        pl.loop(1, levs)(lambda k: act(lax.rem(lev + k, levs)))

    def select(c):
        @pl.loop(0, number)
        def _(i):
            picked[c][i // per, lax.rem(i, per)] = lands[c][senders[i]]

        blocks[c][lev] = picked[c][lev]

    def solve(c):
        start, tiles, size = chunks[c]
        extra = c == last and rest > 0
        wide = (tiles + extra) * LANES
        row = lax.broadcasted_iota(jnp.int32, (levels, LANES), 0)
        lane = lax.broadcasted_iota(jnp.int32, (levels, LANES), 1)
        belongs = lane // max(rest, 1) == row
        first = lax.broadcasted_iota(jnp.int32, (LANES, LANES), 0)
        second = lax.broadcasted_iota(jnp.int32, (LANES, LANES), 1)

        def exact(a, b):
            return jnp.dot(
                a, b, precision=lax.Precision.HIGHEST, preferred_element_type=jnp.float32
            )

        @pl.loop(0, per)
        def _(p):
            for b in range(levs):
                rows = pl.ds(b * levels, levels)
                for t in range(tiles):
                    matrix[rows, pl.ds(t * LANES, LANES)] = blocks[c][
                        b, p, pl.ds(t, levels, stride=tiles), :
                    ]
                if extra:
                    line = blocks[c][b, p, pl.ds(levels * tiles, 1), :]
                    matrix[rows, pl.ds(tiles * LANES, LANES)] = jnp.where(belongs, line, 0.0)
            if extra:
                fold = (first % rest == second) & (first < levels * rest)
                edges = pl.ds(tiles * LANES, LANES)
                matrix[:, edges] = exact(matrix[:, edges], fold.astype(jnp.float32))
            modes = exact(to_modes[...], matrix[:, pl.ds(0, wide)])
            column = start * LANES + lax.broadcasted_iota(jnp.int32, (1, wide), 1)
            within = jnp.where(column >= PLEN, column - PLEN, column)
            pair = me * number + lev * per + p
            degree = jnp.where(within <= NT - pair, pair + within, within - 1)
            ratio = (degree * (degree + 1)).astype(jnp.float32) / float(NT * (NT + 1))
            scaled = modes / (1.0 + depth[...] * ratio)
            matrix[:, pl.ds(0, wide)] = exact(from_modes[...], scaled)
            if extra:
                spread = (second % rest == first) & (second < levels * rest)
                edges = pl.ds(tiles * LANES, LANES)
                matrix[:, edges] = exact(matrix[:, edges], spread.astype(jnp.float32))
            for b in range(levs):
                rows = pl.ds(b * levels, levels)
                base = (b * per + p) * size
                for t in range(tiles):
                    backs[c][pl.ds(base + t, levels, stride=tiles), :] = matrix[
                        rows, pl.ds(t * LANES, LANES)
                    ]
                if extra:
                    line = jnp.where(belongs, matrix[rows, pl.ds(tiles * LANES, LANES)], 0.0)
                    backs[c][pl.ds(base + levels * tiles, 1), :] = jnp.sum(
                        line, axis=0, keepdims=True
                    )

        own = pl.ds(pl.multiple_of(lev * per * size, 8), per * size)
        homes[c][own] = backs[c][own]

    def unpack(c):
        start, tiles, size = chunks[c]

        @pl.loop(0, levels)
        def _(l):
            rows = pl.ds(pl.multiple_of(l * number, number), number)
            for t in range(tiles):
                result[start + t, rows, :] = homes[c][pl.ds(l * tiles + t, number, stride=size), :]

        if c == last and rest:
            edge_out[...] = homes[c][pl.ds(levels * tiles, number, stride=size), :]

    for c in range(n):
        each_tile(c, lambda c, t: load(c, t).start())
    barrier = pltpu.get_barrier_semaphore()

    @pl.loop(1, waves)
    def _(k):
        pl.semaphore_signal(
            barrier, inc=1, device_id={"wave": lax.rem(me + k, waves)}, device_id_type=MESH
        )

    @pl.loop(1, levs)
    def _(k):
        pl.semaphore_signal(
            barrier, inc=1, device_id={"lev": lax.rem(lev + k, levs)}, device_id_type=MESH
        )

    each_tile(0, lambda c, t: load(c, t).wait())
    gather(0)
    pl.semaphore_wait(barrier, waves + levs - 2)
    each_wave(lambda k: wave_copy(0, k).start())
    lands[0][me] = packs[0][me]
    for c in range(1, n):
        each_tile(c, lambda c, t: load(c, t).wait())
        gather(c)
        lands[c][me] = packs[c][me]

    for c in range(n):
        if c < last:

            def follow(k, c=c):
                wave_copy(c, k).wait_send()
                wave_copy(c + 1, k).start()

            each_wave(follow)
        else:
            each_wave(lambda k, c=c: wave_copy(c, k).wait_send())
        each_wave(lambda k, c=c: wave_copy(c, k, True).wait_recv())
        select(c)
        each_lev(lambda j, c=c: modal(c, j, lev).start())
        each_lev(lambda j, c=c: modal(c, j, j).wait_recv())
        solve(c)
        each_lev(lambda j, c=c: back(c, j, lev).start())
        if c > 0:
            each_lev(lambda j, c=c: back(c - 1, j, j).wait_recv())
            unpack(c - 1)
            each_tile(c - 1, lambda c, t: store(c, t).start())
    each_lev(lambda j: back(last, j, j).wait_recv())
    unpack(last)
    each_tile(last, lambda c, t: store(c, t).start())
    for c in range(n):
        each_lev(lambda j, c=c: modal(c, j, j).wait_send())
        each_lev(lambda j, c=c: back(c, j, j).wait_send())
        each_tile(c, lambda c, t: store(c, t).wait())


def per_device(waves, levs, spectral, to_modes, from_modes, depth, owner):
    levels, slots, width = spectral.shape
    number = owner.shape[0] // waves
    per = number // levs
    me = lax.axis_index("wave")
    mine = jnp.sum((owner.reshape(waves, number) == me).astype(jnp.int32), axis=1)
    order = jnp.arange(waves, dtype=jnp.int32)
    before = jnp.where(order[None, :] < order[:, None], mine[None, :], 0)
    picks = jnp.minimum(jnp.sum(before, axis=1), slots - 1)
    senders = lax.dynamic_slice_in_dim(owner, me * number, number)

    tiles, rest = divmod(width, LANES)
    edge = spectral[:, :, tiles * LANES :].transpose(1, 0, 2).reshape(slots, levels * rest)
    edge = jnp.pad(edge, ((0, 0), (0, LANES - levels * rest)))
    n = len(SIZES)
    chunks = []
    for c, size in enumerate(SIZES):
        start = sum(SIZES[:c])
        chunks.append((start, size, rows_of(levels, size, rest if c == n - 1 else 0)))
    largest = max(SIZES) * LANES

    def buffers(*lead):
        return [pltpu.VMEM((*lead, r, LANES), jnp.float32) for _, _, r in chunks]

    flat = [pltpu.VMEM((number * r, LANES), jnp.float32) for _, _, r in chunks]
    vmem = pl.BlockSpec(memory_space=pltpu.VMEM)
    smem = pl.BlockSpec(memory_space=pltpu.SMEM)
    hbm = pl.BlockSpec(memory_space=pl.ANY)
    dma = pltpu.SemaphoreType.DMA
    body, side = pl.pallas_call(
        functools.partial(kernel, waves, levs, number, levels, slots, rest, chunks),
        out_shape=(
            jax.ShapeDtypeStruct((levels * number, tiles * LANES), jnp.float32),
            jax.ShapeDtypeStruct((number, LANES), jnp.float32),
        ),
        in_specs=[smem, smem, hbm, vmem, vmem, vmem, vmem],
        out_specs=(hbm, vmem),
        scratch_shapes=[
            [pltpu.VMEM((size, levels * slots, LANES), jnp.float32) for size in SIZES],
            pltpu.VMEM((tiles, levels * number, LANES), jnp.float32),
            pltpu.VMEM((levels * levs, largest), jnp.float32),
            buffers(waves), buffers(waves), buffers(levs, per), buffers(levs, per),
            flat, flat,
            dma((tiles,)), dma((tiles,)), dma((n, waves)), dma((n, waves)),
            dma((n, levs)), dma((n, levs)), dma((n, levs)), dma((n, levs)),
        ],
        compiler_params=pltpu.CompilerParams(
            collective_id=0, has_side_effects=True, vmem_limit_bytes=60 * 2**20
        ),
        name="helmholtz",
    )(picks, senders, spectral.reshape(levels * slots, width), edge, to_modes, from_modes,
      depth.reshape(-1, 1))
    side = side[:, : levels * rest].reshape(number, levels, rest).transpose(1, 0, 2)
    return jnp.concatenate([body.reshape(levels, number, tiles * LANES), side], axis=2)


def solution(mesh):
    placed = (P("lev", "wave", None), P(), P(), P(), P())
    step = functools.partial(per_device, mesh.shape["wave"], mesh.shape["lev"])
    return jax.shard_map(
        step, mesh=mesh, in_specs=placed, out_specs=P("lev", "wave", None), check_vma=False
    )
```

time: 320 us -> 186 us (0.58)
  Pallas kernels: 0 us -> 172 us
  waiting for transfers between devices: 172 us -> 0 us
  blocking collectives: 49.7 us -> 0 us
  local copies, waits for them, and re-layouts: 48.4 us -> 5.58 us
  starting transfers between devices: 24.2 us -> 0 us
  other arithmetic: 15.3 us -> 5.09 us
  matrix products: 6.02 us -> 0 us
    pallas_call x0 -> x1, Pallas kernels: none -> 172 us  [per_device(): pl.pallas_call(functools.partial(kernel, waves, levs, number, levels, slo...]
    all_to_all x3 -> x0, waiting for transfers between devices: 172 us -> none  [the longest x2 125 us: exchange_in_pieces(): lax.all_to_all(share, axis, split_axis=0, concat_axis=0, tiled=True)]
    all_to_all x1 -> x0, blocking collectives: 49.7 us -> none  [per_device(): lax.all_to_all(mixed, 'lev', split_axis=0, concat_axis=1, tiled=True)]
    all_to_all x3 -> x0, starting transfers between devices: 24.2 us -> none  [the longest x2 18.6 us: exchange_in_pieces(): lax.all_to_all(share, axis, split_axis=0, concat_axis=0, tiled=True)]
    gather x4 -> x0, local copies, waits for them, and re-layouts: 22.4 us -> none  [the longest x1 11.3 us: per_device(): outgoing = jnp.take(spectral, picks, axis=1)]
    split x5 -> x0, local copies, waits for them, and re-layouts: 9.99 us -> none  [exchange_in_pieces(): jnp.split(parts, cut_rows(parts.shape[split_at], pieces), axis=split_at)]
    all_to_all x4 -> x0, local copies, waits for them, and re-layouts: 8.3 us -> none  [the longest x1 2.95 us: exchange_in_pieces(): lax.all_to_all(share, axis, split_axis=0, concat_axis=0, tiled=True)]
    reshape x1 -> x0, other arithmetic: 7.13 us -> none  [joined_along(): parts.reshape(*lengths[:dim], lengths[dim] * lengths[dim + 1], *lengths[d...]
  transfers between devices with their start and end apart: 3 -> 0, of which waited for: 3 -> 0; matrix products, arithmetic and copies ran while one was open for 2% -> 0% of each run, Pallas kernels for 0% -> 0%
where the time goes in v1:
time: 186 us; the launch traced here: 183 us
  Pallas kernels  172 us (92%)
  local copies, waits for them, and re-layouts  5.58 us (3%)
  other arithmetic  5.09 us (3%)
    pallas_call x1, Pallas kernels, per_device(): pl.pallas_call(functools.partial(kernel, waves, levs, number, levels, slo...  172 us

profile of v1, /device:TPU:3, one launch (start us, length us, event | category | flops | bytes accessed | tf_op | source)
XLA Modules:
  0.0 182.7 jit_solution(7662089660849156106)
XLA Ops:
  0.0 1.3 dynamic_slice.3.senders
  1.3 0.7 compare_convert_fusion
  1.9 0.1 reshape.26
  2.0 0.1 reduce_sum.18
  2.1 0.1 select_reduce_fusion
  2.3 0.6 broadcast_minimum_fusion.picks
  2.8 1.4 copy.15.depth
  4.2 1.0 slice_bitcast_fusion
  5.2 0.2 copy.13
  5.4 0.1 copy.14
  5.5 0.6 pad.4.edge
  6.1 172.0 %helmholtz.1 = (f32[272,2560]{1,0:T(8,128)}, f32[16,128]{1,0:T(8,128)}) custom-call(s32[32]{0:T(128)} %broadcast_minimum_fusion.picks, s32[16]{0:T(128)} %dynamic_slice.3.senders, f32[544,2562]{1,0:T(8,128)} %bitcast.11, f32[32,128]{1,0:T(8,128)} %pad.4.edge, f32[136,136]{1,0:T(8,128)} %to_modes.1, f32[136,136]{1,0:T(8,128)} %from_modes.1, f32[136,1]{1,0:T(8,128)} %copy.15.depth), custom_call_target="tpu_custom_call" | custom-call | tf_op jit(solution)/shard_map/helmholtz/pallas_call | solution.py:257
  178.1 0.8 copy.16
  178.9 0.2 copy.17
  179.1 3.6 %pad_maximum_fusion = f32[17,16,2562]{2,1,0:T(8,128)} fusion(f32[17,16,2]{2,1,0:T(8,128)S(1)} %copy.17, f32[17,16,2560]{2,1,0:T(8,128)} %bitcast.12), kind=kLoop, calls=%fused_computation | loop fusion | flops 696864 | bytes 5574912 | tf_op jit(solution)/shard_map/concatenate | solution.py:281
  (2 shorter events, 0.0 us)

commit v2 on v1

v2 whole, which is shorter than its diff:
```python
import functools

import jax
import jax.numpy as jnp
from jax import lax
from jax.experimental import pallas as pl
from jax.experimental.pallas import tpu as pltpu
from jax.sharding import PartitionSpec as P

NT = 1279
PLEN = NT + 2
LANES = 128
SPANS = ((0, 8), (16, 4), (8, 8))
EDGE = 1
SPREAD = 4
HALVES = 2
MESH = pl.DeviceIdType.MESH


def rows_of(levels, tiles, rest):
    return -(-(levels * tiles + (rest > 0)) // 8) * 8


def kernel(
    waves, levs, number, levels, slots, rest, chunks,
    owner, spectral, border, to_modes, from_modes, depth, out,
    picks, pairs, held, edge, result, matrix, packs, lands, picked, blocks, backs, homes,
    in_sem, out_sem, send1, recv1, send2, recv2, send3, recv3, send4, recv4,
):
    me = lax.axis_index("wave")
    lev = lax.axis_index("lev")
    per = number // levs
    planes = waves // SPREAD
    n = len(chunks)
    early = n - 1
    sub = chunks[early][1] // HALVES
    lane = lax.rem(lev, 2) * 2 + lax.rem(lev // 2, 2)
    half = lev // SPREAD

    def solver(place, h):
        return (h * 2 + lax.rem(place, 2)) * 2 + place // 2

    def load(c, t):
        at = chunks[c][0] + t
        return pltpu.make_async_copy(
            spectral.at[:, pl.ds(at * LANES, LANES)], held[c].at[t], in_sem.at[at]
        )

    def each_tile(c, act):
        for t in range(chunks[c][1]):
            act(c, t)

    def each_wave(act):
        pl.loop(1, waves)(lambda k: act(lax.rem(me + k, waves)))

    def each_lev(act):
        pl.loop(1, levs)(lambda k: act(lax.rem(lev + k, levs)))

    def each_far(act):
        @pl.loop(0, planes * levs)
        def _(k):
            plane = lax.rem(me // SPREAD + 3 * k, planes)
            b = lax.rem(half * SPREAD + lax.rem(me, SPREAD) + k // planes, levs)
            away = jnp.logical_or(b != lev, plane * SPREAD + lane != me)
            pl.when(away)(lambda: act(b, plane))

    def each_source(act):
        @pl.loop(0, waves)
        def _(k):
            s = lax.rem(me + k, waves)
            for h in range(HALVES):
                j = solver(lax.rem(me, SPREAD), h)
                pl.when(jnp.logical_or(s != me, lev != j))(lambda h=h, j=j: act(s, h, j))

    def wave_copy(c, peer, at):
        return pltpu.make_async_remote_copy(
            src_ref=packs[c].at[peer], dst_ref=lands[c].at[at],
            send_sem=send1.at[c, peer], recv_sem=recv1.at[c, at],
            device_id={"wave": peer}, device_id_type=MESH,
        )

    def part(ref, at, size):
        return ref.at[pl.ds(pl.multiple_of(at * size, 8), size)]

    def far_copy(b, plane, at):
        return pltpu.make_async_remote_copy(
            src_ref=backs[early].at[b * planes + plane], dst_ref=lands[early].at[at],
            send_sem=send4.at[b * planes + plane], recv_sem=recv4.at[at],
            device_id={"wave": plane * SPREAD + lane, "lev": b}, device_id_type=MESH,
        )

    def modal(c, peer, at):
        source = packs[c] if c == early else picked[c]
        return pltpu.make_async_remote_copy(
            src_ref=source.at[peer], dst_ref=blocks[c].at[at],
            send_sem=send2.at[c, peer], recv_sem=recv2.at[c, at],
            device_id={"lev": peer}, device_id_type=MESH,
        )

    def back(c, peer, at):
        size = per * chunks[c][2]
        return pltpu.make_async_remote_copy(
            src_ref=part(backs[c], peer, size), dst_ref=part(homes[c], at, size),
            send_sem=send3.at[c, peer], recv_sem=recv3.at[c, at],
            device_id={"lev": peer}, device_id_type=MESH,
        )

    def rank():
        def step(d, count):
            hits = jnp.int32(0)
            pair = jnp.int32(0)
            for i in range(number):
                hit = (owner[d * number + i] == me).astype(jnp.int32)
                hits = hits + hit
                pair = pair + hit * (d * number + i)
            picks[d] = jnp.minimum(count, slots - 1)
            pairs[d] = pair
            return count + hits

        lax.fori_loop(0, waves, step, jnp.int32(0))

    def border_rows():
        total = jnp.zeros((slots, LANES), jnp.float32)
        lane = lax.broadcasted_iota(jnp.int32, (slots, LANES), 1)
        for l in range(levels):
            line = jnp.where(lane < rest, border[pl.ds(l * slots, slots), :], 0.0)
            total = total + (pltpu.roll(line, l * rest, 1) if l else line)
        edge[...] = total

    def gather(c):
        tiles = chunks[c][1]

        @pl.loop(0, waves)
        def _(d):
            rows = pl.ds(picks[d], levels, stride=slots)
            if c == early:
                for h in range(HALVES):
                    target = packs[c].at[solver(lax.rem(d, SPREAD), h), d // SPREAD]
                    for t in range(sub):
                        target[pl.ds(t, levels, stride=sub), :] = held[c][h * sub + t, rows, :]
                return
            for t in range(tiles):
                packs[c][d, pl.ds(t, levels, stride=tiles), :] = held[c][t, rows, :]
            if c == EDGE:
                packs[c][d, pl.ds(levels * tiles, 1), :] = edge[pl.ds(picks[d], 1), :]

    def select(c):
        @pl.loop(0, number)
        def _(i):
            picked[c][i // per, lax.rem(i, per)] = lands[c][owner[me * number + i]]

        blocks[c][lev] = picked[c][lev]

    def solve(c):
        start, tiles, size = chunks[c]
        count = per
        if c == early:
            start, tiles, count = start + half * sub, sub, planes
        extra = c == EDGE
        wide = (tiles + extra) * LANES
        row = lax.broadcasted_iota(jnp.int32, (levels, LANES), 0)
        belongs = lax.broadcasted_iota(jnp.int32, (levels, LANES), 1) // rest == row
        first = lax.broadcasted_iota(jnp.int32, (LANES, LANES), 0)
        second = lax.broadcasted_iota(jnp.int32, (LANES, LANES), 1)
        square = (levels * levs, levels * levs)
        diagonal = lax.broadcasted_iota(jnp.int32, square, 0) == lax.broadcasted_iota(
            jnp.int32, square, 1
        )
        factor = jnp.sum(jnp.where(diagonal, depth[...], 0.0), axis=1, keepdims=True)

        def exact(a, b):
            return jnp.dot(
                a, b, precision=lax.Precision.HIGHEST, preferred_element_type=jnp.float32
            )

        @pl.loop(0, count)
        def _(p):
            for b in range(levs):
                rows = pl.ds(b * levels, levels)
                for t in range(tiles):
                    matrix[rows, pl.ds(t * LANES, LANES)] = blocks[c][
                        b, p, pl.ds(t, levels, stride=tiles), :
                    ]
                if extra:
                    line = blocks[c][b, p, pl.ds(levels * tiles, 1), :]
                    matrix[rows, pl.ds(tiles * LANES, LANES)] = jnp.where(belongs, line, 0.0)
            if extra:
                fold = (first % rest == second) & (first < levels * rest)
                edges = pl.ds(tiles * LANES, LANES)
                matrix[:, edges] = exact(matrix[:, edges], fold.astype(jnp.float32))
            modes = exact(to_modes[...], matrix[:, pl.ds(0, wide)])
            column = start * LANES + lax.broadcasted_iota(jnp.int32, (1, wide), 1)
            within = jnp.where(column >= PLEN, column - PLEN, column)
            pair = pairs[p * SPREAD + lane] if c == early else me * number + lev * per + p
            degree = jnp.where(within <= NT - pair, pair + within, within - 1)
            ratio = (degree * (degree + 1)).astype(jnp.float32) / float(NT * (NT + 1))
            scaled = modes / (1.0 + factor * ratio)
            matrix[:, pl.ds(0, wide)] = exact(from_modes[...], scaled)
            if extra:
                spread = (second % rest == first) & (second < levels * rest)
                edges = pl.ds(tiles * LANES, LANES)
                matrix[:, edges] = exact(matrix[:, edges], spread.astype(jnp.float32))
            for b in range(levs):
                rows = pl.ds(b * levels, levels)
                at = b * count + p
                for t in range(tiles):
                    block = matrix[rows, pl.ds(t * LANES, LANES)]
                    if c == early:
                        backs[c][at, pl.ds(t, levels, stride=tiles), :] = block
                    else:
                        backs[c][pl.ds(at * size + t, levels, stride=tiles), :] = block
                if extra:
                    line = jnp.where(belongs, matrix[rows, pl.ds(tiles * LANES, LANES)], 0.0)
                    backs[c][pl.ds(at * size + levels * tiles, 1), :] = jnp.sum(
                        line, axis=0, keepdims=True
                    )

        if c != early:
            own = pl.ds(pl.multiple_of(lev * per * size, 8), per * size)
            homes[c][own] = backs[c][own]

    def unpack(c, h=0):
        start, tiles, size = chunks[c]
        if c == early:
            start, tiles = start + h * sub, sub

        @pl.loop(0, levels)
        def _(l):
            rows = pl.ds(pl.multiple_of(l * number, number), number)
            for t in range(tiles):
                result[rows, pl.ds((start + t) * LANES, LANES)] = homes[c][
                    pl.ds(l * tiles + t, number, stride=size), :
                ]

        if c == EDGE:
            line = homes[c][pl.ds(levels * tiles, number, stride=size), :]
            for l in range(levels):
                turned = pltpu.roll(line, LANES - l * rest, 1) if l else line
                result[pl.ds(l * number, number), pl.ds((start + tiles) * LANES, rest)] = turned[
                    :, :rest
                ]

    for c in (0, early, *range(1, early)):
        each_tile(c, lambda c, t: load(c, t).start())
    barrier = pltpu.get_barrier_semaphore()

    def greet(**where):
        pl.semaphore_signal(barrier, inc=1, device_id=where, device_id_type=MESH)

    each_wave(lambda d: greet(wave=d))
    each_lev(lambda b: greet(lev=b))
    each_far(lambda b, plane: greet(wave=plane * SPREAD + lane, lev=b))
    each_source(lambda s, h, j: greet(wave=s, lev=j))
    rank()
    each_tile(0, lambda c, t: load(c, t).wait())
    gather(0)
    own = (lane == lax.rem(me, SPREAD)).astype(jnp.int32)
    pl.semaphore_wait(barrier, waves + levs - 2 + 2 * (HALVES * waves - own))
    each_wave(lambda d: wave_copy(0, d, me).start())
    lands[0][me] = packs[0][me]

    each_tile(early, lambda c, t: load(c, t).wait())
    gather(early)
    each_lev(lambda b: modal(early, b, lev).start())
    blocks[early][lev] = packs[early][lev]
    border_rows()
    for c in range(1, early):
        each_tile(c, lambda c, t: load(c, t).wait())
        gather(c)
        each_wave(lambda d, c=c: wave_copy(c, d, me).start())
        lands[c][me] = packs[c][me]
    each_lev(lambda b: modal(early, b, b).wait_recv())
    solve(early)
    each_far(lambda b, plane: far_copy(b, plane, me * HALVES + half).start())

    @pl.when(own == 1)
    def _():
        lands[early][me * HALVES + half] = backs[early][lev * planes + me // SPREAD]

    def finish(c):
        each_lev(lambda b: back(c, b, b).wait_recv())
        unpack(c)

    for c in range(early):
        each_wave(lambda d, c=c: wave_copy(c, d, d).wait_recv())
        select(c)
        each_lev(lambda b, c=c: modal(c, b, lev).start())
        if c > 0:
            finish(c - 1)
        each_lev(lambda b, c=c: modal(c, b, b).wait_recv())
        solve(c)
        each_lev(lambda b, c=c: back(c, b, lev).start())
    finish(early - 1)
    each_source(lambda s, h, j: far_copy(lev, 0, s * HALVES + h).wait_recv())
    for h in range(HALVES):

        @pl.loop(0, number)
        def _(i):
            size = chunks[early][2]
            homes[early][pl.ds(pl.multiple_of(i * size, 8), levels * sub)] = lands[early][
                owner[me * number + i] * HALVES + h
            ]

        unpack(early, h)
    copy = pltpu.make_async_copy(result, out, out_sem)
    copy.start()
    for c in range(n):
        each_lev(lambda b, c=c: modal(c, b, b).wait_send())
        if c != early:
            each_wave(lambda d, c=c: wave_copy(c, d, d).wait_send())
            each_lev(lambda b, c=c: back(c, b, b).wait_send())
    each_far(lambda b, plane: far_copy(b, plane, 0).wait_send())
    copy.wait()


def per_device(waves, levs, spectral, to_modes, from_modes, depth, owner):
    levels, slots, width = spectral.shape
    number = owner.shape[0] // waves
    per, planes = number // levs, waves // SPREAD
    tiles, rest = divmod(width, LANES)
    n = len(SPANS)
    early = n - 1
    chunks = [
        (start, size, rows_of(levels, size if c < early else size // HALVES, rest * (c == EDGE)))
        for c, (start, size) in enumerate(SPANS)
    ]
    packed = levels * SPANS[early][1] // HALVES
    largest = max(size + (c == EDGE) for c, (_, size) in enumerate(SPANS)) * LANES

    def buffers(*lead, last=()):
        rows = [r for _, _, r in chunks[:early]]
        shapes = [(*lead, r, LANES) for r in rows] + ([(*last, packed, LANES)] if last else [])
        return [pltpu.VMEM(shape, jnp.float32) for shape in shapes]

    flat = [pltpu.VMEM((number * r, LANES), jnp.float32) for _, _, r in chunks]
    vmem = pl.BlockSpec(memory_space=pltpu.VMEM)
    smem = pl.BlockSpec(memory_space=pltpu.SMEM)
    hbm = pl.BlockSpec(memory_space=pl.ANY)
    dma = pltpu.SemaphoreType.DMA
    whole = spectral.reshape(levels * slots, width)
    result = pl.pallas_call(
        functools.partial(kernel, waves, levs, number, levels, slots, rest, chunks),
        out_shape=jax.ShapeDtypeStruct((levels * number, width), jnp.float32),
        in_specs=[
            smem, hbm, pl.BlockSpec((levels * slots, LANES), lambda i: (0, tiles)), vmem, vmem, vmem,
        ],
        grid=(1,),
        out_specs=hbm,
        scratch_shapes=[
            pltpu.SMEM((waves,), jnp.int32), pltpu.SMEM((waves,), jnp.int32),
            [pltpu.VMEM((size, levels * slots, LANES), jnp.float32) for _, size in SPANS],
            pltpu.VMEM((slots, LANES), jnp.float32),
            pltpu.VMEM((levels * number, width), jnp.float32),
            pltpu.VMEM((levels * levs, largest), jnp.float32),
            buffers(waves, last=(levs, planes)),
            buffers(waves, last=(HALVES * waves,)),
            buffers(levs, per),
            buffers(levs, per, last=(levs, planes)),
            [*flat[:early], pltpu.VMEM((levs * planes, packed, LANES), jnp.float32)],
            flat,
            dma((tiles,)), dma, dma((n, waves)), dma((n, waves)),
            dma((n, levs)), dma((n, levs)), dma((n, levs)), dma((n, levs)),
            dma((levs * planes,)), dma((HALVES * waves,)),
        ],
        compiler_params=pltpu.CompilerParams(
            collective_id=0, has_side_effects=True, vmem_limit_bytes=62 * 2**20
        ),
        name="helmholtz",
    )(owner, whole, whole, to_modes, from_modes, depth.reshape(1, -1))
    return result.reshape(levels, number, width)


def solution(mesh):
    placed = (P("lev", "wave", None), P(), P(), P(), P())
    step = functools.partial(per_device, mesh.shape["wave"], mesh.shape["lev"])
    return jax.shard_map(
        step, mesh=mesh, in_specs=placed, out_specs=P("lev", "wave", None), check_vma=False
    )
```

time: 186 us -> 173 us (0.930)
  the two profiles are of different devices: /device:TPU:3 before, /device:TPU:6 now
where the time goes in v2:
time: 173 us
  Pallas kernels  170 us (98%)
  local copies, waits for them, and re-layouts  3.61 us (2%)
    pallas_call x1, Pallas kernels, per_device(): pl.pallas_call(functools.partial(kernel, waves, levs, number, levels, slo...  170 us
    unnamed x1, local copies, waits for them, and re-layouts  3.61 us

profile of v2, /device:TPU:6, one launch (start us, length us, event | category | flops | bytes accessed | tf_op | source)
XLA Modules:
  0.0 173.1 jit_solution(5569284869529033409)
XLA Ops:
  0.0 169.5 %helmholtz.1 = f32[272,2562]{1,0:T(8,128)} custom-call(s32[512]{0:T(512)} %owner.1, f32[544,2562]{1,0:T(8,128)} %bitcast.3, f32[544,2562]{1,0:T(8,128)} %bitcast.4, f32[136,136]{1,0:T(8,128)} %to_modes.1, f32[136,136]{1,0:T(8,128)} %from_modes.1, f32[1,136]{1,0:T(1,128)} %bitcast.6), custom_call_target="tpu_custom_call" | custom-call | tf_op jit(solution)/shard_map/helmholtz/pallas_call | solution.py:341
  169.5 3.6 %copy.7 = f32[17,16,2562]{2,1,0:T(8,128)} copy(f32[17,16,2562]{2,1,0:T(8,128)} %bitcast.5) | data formatting | bytes 5574912

commit v3 on v2

v3 whole, which is shorter than its diff:
```python
import functools

import jax
import jax.numpy as jnp
from jax import lax
from jax.experimental import pallas as pl
from jax.experimental.pallas import tpu as pltpu
from jax.sharding import PartitionSpec as P

NT = 1279
PLEN = NT + 2
LANES = 128
SPANS = ((16, 4), (0, 6), (6, 4), (10, 6))
EDGE = 0
SPREAD = 4
HALVES = 2
MESH = pl.DeviceIdType.MESH


def rows_of(levels, tiles, rest):
    return -(-(levels * tiles + (rest > 0)) // 2) * 2


def kernel(
    waves, levs, number, levels, slots, rest, chunks,
    owner, spectral, border, to_modes, from_modes, depth, out,
    picks, pairs, held, edge, result, matrix, packs, lands, picked, blocks, backs, homes,
    in_sem, out_sem, send1, recv1, send2, recv2, send3, recv3, send4, recv4,
):
    me = lax.axis_index("wave")
    lev = lax.axis_index("lev")
    planes = waves // SPREAD
    lines = levs // HALVES
    share = number // lines
    n = len(chunks)
    early = n - 1
    row = lev // HALVES
    side = lax.rem(lev, HALVES)
    lane = (1 - side) * 2 + lax.rem(row, 2)
    half = lev // SPREAD

    def solver(place, h):
        return (h * 2 + lax.rem(place, 2)) * 2 + 1 - place // 2

    def load(c, t):
        at = chunks[c][0] + t
        return pltpu.make_async_copy(
            spectral.at[:, pl.ds(at * LANES, LANES)], held[c].at[t], in_sem.at[at]
        )

    def each_tile(c, act):
        for t in range(HALVES * chunks[c][1]):
            act(c, t)

    def each_wave(act):
        @pl.loop(0, waves)
        def _(k):
            d = lax.rem(me + k, waves)
            for x in range(HALVES):
                pl.when(jnp.logical_or(d != me, side != x))(lambda x=x: act(d, x))

    def each_row(act):
        pl.loop(1, lines)(lambda k: act(lax.rem(row + k, lines)))

    def each_lev(act):
        pl.loop(1, levs)(lambda k: act(lax.rem(lev + k, levs)))

    def each_far(act):
        @pl.loop(0, planes * levs)
        def _(k):
            plane = lax.rem(me // SPREAD + 3 * k, planes)
            b = lax.rem(half * SPREAD + lax.rem(me, SPREAD) + k // planes, levs)
            away = jnp.logical_or(b != lev, plane * SPREAD + lane != me)
            pl.when(away)(lambda: act(b, plane))

    def each_source(act):
        @pl.loop(0, waves)
        def _(k):
            s = lax.rem(me + k, waves)
            for h in range(HALVES):
                j = solver(lax.rem(me, SPREAD), h)
                pl.when(jnp.logical_or(s != me, lev != j))(lambda h=h, j=j: act(s, h, j))

    def wave_copy(c, d, x, at):
        return pltpu.make_async_remote_copy(
            src_ref=packs[c].at[d * HALVES + x], dst_ref=lands[c].at[at],
            send_sem=send1.at[c, d * HALVES + x], recv_sem=recv1.at[c, at],
            device_id={"wave": d, "lev": row * HALVES + x}, device_id_type=MESH,
        )

    def wave_start(c):
        each_wave(lambda d, x: wave_copy(c, d, x, me * HALVES + side).start())
        lands[c][me * HALVES + side] = packs[c][me * HALVES + side]

    def part(ref, at, size):
        return ref.at[pl.ds(pl.multiple_of(at * size, 8), size)]

    def far_copy(b, plane, at):
        return pltpu.make_async_remote_copy(
            src_ref=backs[early].at[b * planes + plane], dst_ref=lands[early].at[at],
            send_sem=send4.at[b * planes + plane], recv_sem=recv4.at[at],
            device_id={"wave": plane * SPREAD + lane, "lev": b}, device_id_type=MESH,
        )

    def spread(peer, at):
        return pltpu.make_async_remote_copy(
            src_ref=packs[early].at[peer], dst_ref=blocks[early].at[at],
            send_sem=send2.at[early, peer], recv_sem=recv2.at[early, at],
            device_id={"lev": peer}, device_id_type=MESH,
        )

    def modal(c, peer, at):
        return pltpu.make_async_remote_copy(
            src_ref=picked[c].at[peer], dst_ref=blocks[c].at[at],
            send_sem=send2.at[c, peer], recv_sem=recv2.at[c, at],
            device_id={"lev": peer * HALVES + side}, device_id_type=MESH,
        )

    def back(c, peer, at):
        size = share * chunks[c][2]
        place = lax.rem(at, HALVES) * lines + at // HALVES
        return pltpu.make_async_remote_copy(
            src_ref=part(backs[c], peer, size), dst_ref=part(homes[c], place, size),
            send_sem=send3.at[c, peer], recv_sem=recv3.at[c, at],
            device_id={"lev": peer}, device_id_type=MESH,
        )

    def rank():
        def step(d, count):
            hits = jnp.int32(0)
            pair = jnp.int32(0)
            for i in range(number):
                hit = (owner[d * number + i] == me).astype(jnp.int32)
                hits = hits + hit
                pair = pair + hit * (d * number + i)
            picks[d] = jnp.minimum(count, slots - 1)
            pairs[d] = pair
            return count + hits

        lax.fori_loop(0, waves, step, jnp.int32(0))

    def border_rows():
        total = jnp.zeros((slots, LANES), jnp.float32)
        lane = lax.broadcasted_iota(jnp.int32, (slots, LANES), 1)
        for l in range(levels):
            line = jnp.where(lane < rest, border[pl.ds(l * slots, slots), :], 0.0)
            total = total + (pltpu.roll(line, l * rest, 1) if l else line)
        edge[...] = total

    def gather(c):
        sub = chunks[c][1]

        @pl.loop(0, waves)
        def _(d):
            rows = pl.ds(picks[d], levels, stride=slots)
            for h in range(HALVES):
                if c == early:
                    target = packs[c].at[solver(lax.rem(d, SPREAD), h), d // SPREAD]
                else:
                    target = packs[c].at[d * HALVES + h]
                for t in range(sub):
                    target[pl.ds(t, levels, stride=sub), :] = held[c][h * sub + t, rows, :]
                if c == EDGE:
                    target[pl.ds(levels * sub, 1), :] = edge[pl.ds(picks[d], 1), :]

    def select(c):
        @pl.loop(0, number)
        def _(i):
            for x in range(HALVES):
                picked[c][i // share, x * share + lax.rem(i, share)] = lands[c][
                    owner[me * number + i] * HALVES + x
                ]

        blocks[c][row] = picked[c][row]

    def solve(c):
        start, tiles, size = chunks[c]
        start = start + (half if c == early else side) * tiles
        count = planes if c == early else share
        edge_start = (chunks[EDGE][0] + (HALVES - 1) * chunks[EDGE][1]) * LANES
        extra = c == EDGE
        wide = (tiles + extra) * LANES
        level = lax.broadcasted_iota(jnp.int32, (levels, LANES), 0)
        belongs = lax.broadcasted_iota(jnp.int32, (levels, LANES), 1) // rest == level
        first = lax.broadcasted_iota(jnp.int32, (LANES, LANES), 0)
        second = lax.broadcasted_iota(jnp.int32, (LANES, LANES), 1)
        square = (levels * levs, levels * levs)
        diagonal = lax.broadcasted_iota(jnp.int32, square, 0) == lax.broadcasted_iota(
            jnp.int32, square, 1
        )
        factor = jnp.sum(jnp.where(diagonal, depth[...], 0.0), axis=1, keepdims=True)

        def exact(a, b):
            return jnp.dot(
                a, b, precision=lax.Precision.HIGHEST, preferred_element_type=jnp.float32
            )

        @pl.loop(0, count)
        def _(p):
            for b in range(levs):
                rows = pl.ds(b * levels, levels)
                block = blocks[c].at[b, p]
                if c != early:
                    block = blocks[c].at[b // HALVES, b % HALVES * share + p]
                for t in range(tiles):
                    matrix[rows, pl.ds(t * LANES, LANES)] = block[
                        pl.ds(t, levels, stride=tiles), :
                    ]
                if extra:
                    line = block[pl.ds(levels * tiles, 1), :]
                    matrix[rows, pl.ds(tiles * LANES, LANES)] = jnp.where(belongs, line, 0.0)
            if extra:
                fold = (first % rest == second) & (first < levels * rest)
                edges = pl.ds(tiles * LANES, LANES)
                matrix[:, edges] = exact(matrix[:, edges], fold.astype(jnp.float32))
            modes = exact(to_modes[...], matrix[:, pl.ds(0, wide)])
            column = lax.broadcasted_iota(jnp.int32, (1, wide), 1)
            column = jnp.where(column < tiles * LANES, start * LANES, edge_start) + column
            within = jnp.where(column >= PLEN, column - PLEN, column)
            pair = pairs[p * SPREAD + lane] if c == early else me * number + row * share + p
            degree = jnp.where(within <= NT - pair, pair + within, within - 1)
            ratio = (degree * (degree + 1)).astype(jnp.float32) / float(NT * (NT + 1))
            scaled = modes / (1.0 + factor * ratio)
            matrix[:, pl.ds(0, wide)] = exact(from_modes[...], scaled)
            if extra:
                unfold = (second % rest == first) & (second < levels * rest)
                edges = pl.ds(tiles * LANES, LANES)
                matrix[:, edges] = exact(matrix[:, edges], unfold.astype(jnp.float32))
            for b in range(levs):
                rows = pl.ds(b * levels, levels)
                at = b * count + p
                for t in range(tiles):
                    block = matrix[rows, pl.ds(t * LANES, LANES)]
                    if c == early:
                        backs[c][at, pl.ds(t, levels, stride=tiles), :] = block
                    else:
                        backs[c][pl.ds(at * size + t, levels, stride=tiles), :] = block
                if extra:
                    line = jnp.where(belongs, matrix[rows, pl.ds(tiles * LANES, LANES)], 0.0)
                    backs[c][pl.ds(at * size + levels * tiles, 1), :] = jnp.sum(
                        line, axis=0, keepdims=True
                    )

        if c != early:
            area = share * size
            place = pl.multiple_of((side * lines + row) * area, 8)
            homes[c][pl.ds(place, area)] = backs[c][pl.ds(pl.multiple_of(lev * area, 8), area)]

    def unpack(c, h, offset):
        start, tiles, size = chunks[c]
        start = start + h * tiles

        @pl.loop(0, levels)
        def _(l):
            rows = pl.ds(pl.multiple_of(l * number, number), number)
            for t in range(tiles):
                result[rows, pl.ds((start + t) * LANES, LANES)] = homes[c][
                    pl.ds(offset + l * tiles + t, number, stride=size), :
                ]

        if c == EDGE and h == HALVES - 1:
            line = homes[c][pl.ds(offset + levels * tiles, number, stride=size), :]
            for l in range(levels):
                turned = pltpu.roll(line, LANES - l * rest, 1) if l else line
                result[pl.ds(l * number, number), pl.ds((start + tiles) * LANES, rest)] = turned[
                    :, :rest
                ]

    for c in (0, early, *range(1, early)):
        each_tile(c, lambda c, t: load(c, t).start())
    barrier = pltpu.get_barrier_semaphore()

    def greet(**where):
        pl.semaphore_signal(barrier, inc=1, device_id=where, device_id_type=MESH)

    each_wave(lambda d, x: greet(wave=d, lev=row * HALVES + x))
    each_lev(lambda b: greet(lev=b))
    each_far(lambda b, plane: greet(wave=plane * SPREAD + lane, lev=b))
    each_source(lambda s, h, j: greet(wave=s, lev=j))
    rank()
    border_rows()
    each_tile(0, lambda c, t: load(c, t).wait())
    gather(0)
    own = (lane == lax.rem(me, SPREAD)).astype(jnp.int32)
    pl.semaphore_wait(barrier, HALVES * waves + levs - 2 + 2 * (HALVES * waves - own))
    wave_start(0)

    each_tile(early, lambda c, t: load(c, t).wait())
    gather(early)
    each_lev(lambda b: spread(b, lev).start())
    blocks[early][lev] = packs[early][lev]
    for c in range(1, early):
        each_tile(c, lambda c, t: load(c, t).wait())
        gather(c)
        wave_start(c)
    each_lev(lambda b: spread(b, b).wait_recv())
    solve(early)
    each_far(lambda b, plane: far_copy(b, plane, me * HALVES + half).start())

    @pl.when(own == 1)
    def _():
        lands[early][me * HALVES + half] = backs[early][lev * planes + me // SPREAD]

    def finish(c):
        each_lev(lambda b: back(c, b, b).wait_recv())
        for h in range(HALVES):
            unpack(c, h, h * number * chunks[c][2])

    for c in range(early):
        each_wave(lambda d, x, c=c: wave_copy(c, d, x, d * HALVES + x).wait_recv())
        select(c)
        each_row(lambda r, c=c: modal(c, r, row).start())
        if c > 0:
            finish(c - 1)
        each_row(lambda r, c=c: modal(c, r, r).wait_recv())
        solve(c)
        each_lev(lambda b, c=c: back(c, b, lev).start())
    finish(early - 1)
    each_source(lambda s, h, j: far_copy(lev, 0, s * HALVES + h).wait_recv())
    for h in range(HALVES):

        @pl.loop(0, number)
        def _(i):
            size = chunks[early][2]
            homes[early][pl.ds(i * size, size)] = lands[early][
                owner[me * number + i] * HALVES + h
            ]

        unpack(early, h, 0)
    copy = pltpu.make_async_copy(result, out, out_sem)
    copy.start()
    for c in range(early):
        each_wave(lambda d, x, c=c: wave_copy(c, d, x, 0).wait_send())
        each_row(lambda r, c=c: modal(c, r, r).wait_send())
        each_lev(lambda b, c=c: back(c, b, b).wait_send())
    each_lev(lambda b: spread(b, b).wait_send())
    each_far(lambda b, plane: far_copy(b, plane, 0).wait_send())
    copy.wait()


def per_device(waves, levs, spectral, to_modes, from_modes, depth, owner):
    levels, slots, width = spectral.shape
    number = owner.shape[0] // waves
    planes, lines = waves // SPREAD, levs // HALVES
    share = number // lines
    tiles, rest = divmod(width, LANES)
    n = len(SPANS)
    early = n - 1
    chunks = [
        (start, size // HALVES, rows_of(levels, size // HALVES, rest * (c == EDGE)))
        for c, (start, size) in enumerate(SPANS)
    ]
    largest = max(size + (c == EDGE) for c, (_, size, _) in enumerate(chunks)) * LANES

    def buffers(*lead, last=()):
        shapes = [(*lead, r, LANES) for _, _, r in chunks[:early]]
        shapes += [(*last, chunks[early][2], LANES)] if last else []
        return [pltpu.VMEM(shape, jnp.float32) for shape in shapes]

    flat = [pltpu.VMEM((HALVES * number * r, LANES), jnp.float32) for _, _, r in chunks]
    vmem = pl.BlockSpec(memory_space=pltpu.VMEM)
    smem = pl.BlockSpec(memory_space=pltpu.SMEM)
    hbm = pl.BlockSpec(memory_space=pl.ANY)
    dma = pltpu.SemaphoreType.DMA
    whole = spectral.reshape(levels * slots, width)
    result = pl.pallas_call(
        functools.partial(kernel, waves, levs, number, levels, slots, rest, chunks),
        out_shape=jax.ShapeDtypeStruct((levels * number, width), jnp.float32),
        in_specs=[
            smem, hbm, pl.BlockSpec((levels * slots, LANES), lambda i: (0, tiles)), vmem, vmem, vmem,
        ],
        grid=(1,),
        out_specs=hbm,
        scratch_shapes=[
            pltpu.SMEM((waves,), jnp.int32), pltpu.SMEM((waves,), jnp.int32),
            [pltpu.VMEM((size, levels * slots, LANES), jnp.float32) for _, size in SPANS],
            pltpu.VMEM((slots, LANES), jnp.float32),
            pltpu.VMEM((levels * number, width), jnp.float32),
            pltpu.VMEM((levels * levs, largest), jnp.float32),
            buffers(HALVES * waves, last=(levs, planes)),
            buffers(HALVES * waves, last=(HALVES * waves,)),
            buffers(lines, HALVES * share),
            buffers(lines, HALVES * share, last=(levs, planes)),
            [*flat[:early], *buffers(last=(levs * planes,))[early:]],
            flat,
            dma((tiles,)), dma,
            dma((early, HALVES * waves)), dma((early, HALVES * waves)),
            dma((n, levs)), dma((n, levs)), dma((n, levs)), dma((n, levs)),
            dma((levs * planes,)), dma((HALVES * waves,)),
        ],
        compiler_params=pltpu.CompilerParams(
            collective_id=0, has_side_effects=True, vmem_limit_bytes=62 * 2**20
        ),
        name="helmholtz",
    )(owner, whole, whole, to_modes, from_modes, depth.reshape(1, -1))
    return result.reshape(levels, number, width)


def solution(mesh):
    placed = (P("lev", "wave", None), P(), P(), P(), P())
    step = functools.partial(per_device, mesh.shape["wave"], mesh.shape["lev"])
    return jax.shard_map(
        step, mesh=mesh, in_specs=placed, out_specs=P("lev", "wave", None), check_vma=False
    )
```

time: 173 us -> 161 us (0.931)
  the two profiles are of different devices: /device:TPU:6 before, /device:TPU:3 now
where the time goes in v3:
time: 161 us; the launch traced here: 160 us
  Pallas kernels  157 us (98%)
  local copies, waits for them, and re-layouts  3.61 us (2%)
    pallas_call x1, Pallas kernels, per_device(): pl.pallas_call(functools.partial(kernel, waves, levs, number, levels, slo...  157 us
    unnamed x1, local copies, waits for them, and re-layouts  3.61 us

profile of v3, /device:TPU:3, one launch (start us, length us, event | category | flops | bytes accessed | tf_op | source)
XLA Modules:
  0.0 160.4 jit_solution(2679988686930308596)
XLA Ops:
  0.0 156.8 %helmholtz.1 = f32[272,2562]{1,0:T(8,128)} custom-call(s32[512]{0:T(512)} %owner.1, f32[544,2562]{1,0:T(8,128)} %bitcast.3, f32[544,2562]{1,0:T(8,128)} %bitcast.4, f32[136,136]{1,0:T(8,128)} %to_modes.1, f32[136,136]{1,0:T(8,128)} %from_modes.1, f32[1,136]{1,0:T(1,128)} %bitcast.6), custom_call_target="tpu_custom_call" | custom-call | tf_op jit(solution)/shard_map/helmholtz/pallas_call | solution.py:366
  156.8 3.6 %copy.7 = f32[17,16,2562]{2,1,0:T(8,128)} copy(f32[17,16,2562]{2,1,0:T(8,128)} %bitcast.5) | data formatting | bytes 5574912

commit v4 on v3

--- a/solution.py
+++ b/solution.py
@@ -25,7 +25,7 @@
     waves, levs, number, levels, slots, rest, chunks,
     owner, spectral, border, to_modes, from_modes, depth, out,
     picks, pairs, held, edge, result, matrix, packs, lands, picked, blocks, backs, homes,
-    in_sem, out_sem, send1, recv1, send2, recv2, send3, recv3, send4, recv4,
+    in_sem, out_sem, send1, recv1, send2, recv2, send3, recv3, send4, recv4, entered,
 ):
     me = lax.axis_index("wave")
     lev = lax.axis_index("lev")
@@ -275,15 +275,16 @@
 
     each_wave(lambda d, x: greet(wave=d, lev=row * HALVES + x))
     each_lev(lambda b: greet(lev=b))
-    each_far(lambda b, plane: greet(wave=plane * SPREAD + lane, lev=b))
-    each_source(lambda s, h, j: greet(wave=s, lev=j))
     rank()
     border_rows()
     each_tile(0, lambda c, t: load(c, t).wait())
     gather(0)
     own = (lane == lax.rem(me, SPREAD)).astype(jnp.int32)
-    pl.semaphore_wait(barrier, HALVES * waves + levs - 2 + 2 * (HALVES * waves - own))
+    pl.semaphore_wait(barrier, HALVES * waves + levs - 2)
     wave_start(0)
+    each_lev(
+        lambda b: pl.semaphore_signal(entered, inc=1, device_id={"lev": b}, device_id_type=MESH)
+    )
 
     each_tile(early, lambda c, t: load(c, t).wait())
     gather(early)
@@ -295,6 +296,7 @@
         wave_start(c)
     each_lev(lambda b: spread(b, b).wait_recv())
     solve(early)
+    pl.semaphore_wait(entered, levs - 1)
     each_far(lambda b, plane: far_copy(b, plane, me * HALVES + half).start())
 
     @pl.when(own == 1)
@@ -387,6 +389,7 @@
             dma((early, HALVES * waves)), dma((early, HALVES * waves)),
             dma((n, levs)), dma((n, levs)), dma((n, levs)), dma((n, levs)),
             dma((levs * planes,)), dma((HALVES * waves,)),
+            pltpu.SemaphoreType.REGULAR,
         ],
         compiler_params=pltpu.CompilerParams(
             collective_id=0, has_side_effects=True, vmem_limit_bytes=62 * 2**20

time: 161 us -> 159 us (0.988); the launches traced: 160 us -> 156 us
  Pallas kernels: 157 us -> 152 us
    pallas_call x1, Pallas kernels: 157 us -> 152 us  [per_device(): pl.pallas_call(functools.partial(kernel, waves, levs, number, levels, slo...]
where the time goes in v4:
time: 159 us; the launch traced here: 156 us
  Pallas kernels  152 us (96%)
  local copies, waits for them, and re-layouts  3.61 us (2%)
    pallas_call x1, Pallas kernels, per_device(): pl.pallas_call(functools.partial(kernel, waves, levs, number, levels, slo...  152 us
    unnamed x1, local copies, waits for them, and re-layouts  3.61 us

profile of v4, /device:TPU:3, one launch (start us, length us, event | category | flops | bytes accessed | tf_op | source)
XLA Modules:
  0.0 155.8 jit_solution(663910091225712703)
XLA Ops:
  0.0 152.2 %helmholtz.1 = f32[272,2562]{1,0:T(8,128)} custom-call(s32[512]{0:T(512)} %owner.1, f32[544,2562]{1,0:T(8,128)} %bitcast.3, f32[544,2562]{1,0:T(8,128)} %bitcast.4, f32[136,136]{1,0:T(8,128)} %to_modes.1, f32[136,136]{1,0:T(8,128)} %from_modes.1, f32[1,136]{1,0:T(1,128)} %bitcast.6), custom_call_target="tpu_custom_call" | custom-call | tf_op jit(solution)/shard_map/helmholtz/pallas_call | solution.py:368
  152.2 3.6 %copy.7 = f32[17,16,2562]{2,1,0:T(8,128)} copy(f32[17,16,2562]{2,1,0:T(8,128)} %bitcast.5) | data formatting | bytes 5574912

commit v5 on v4

--- a/solution.py
+++ b/solution.py
@@ -55,7 +55,7 @@
     def each_wave(act):
         @pl.loop(0, waves)
         def _(k):
-            d = lax.rem(me + k, waves)
+            d = lax.rem(me + 13 * k, waves)
             for x in range(HALVES):
                 pl.when(jnp.logical_or(d != me, side != x))(lambda x=x: act(d, x))
 

time: 159 us -> 157 us (0.987); the launches traced: 156 us -> 156 us
  no operation moved by 1% of the time
where the time goes in v5:
time: 157 us; the launch traced here: 156 us
  Pallas kernels  153 us (97%)
  local copies, waits for them, and re-layouts  3.61 us (2%)
    pallas_call x1, Pallas kernels, per_device(): pl.pallas_call(functools.partial(kernel, waves, levs, number, levels, slo...  153 us
    unnamed x1, local copies, waits for them, and re-layouts  3.61 us

profile of v5, /device:TPU:3, one launch (start us, length us, event | category | flops | bytes accessed | tf_op | source)
XLA Modules:
  0.0 156.4 jit_solution(14474087220298590797)
XLA Ops:
  0.0 152.8 %helmholtz.1 = f32[272,2562]{1,0:T(8,128)} custom-call(s32[512]{0:T(512)} %owner.1, f32[544,2562]{1,0:T(8,128)} %bitcast.3, f32[544,2562]{1,0:T(8,128)} %bitcast.4, f32[136,136]{1,0:T(8,128)} %to_modes.1, f32[136,136]{1,0:T(8,128)} %from_modes.1, f32[1,136]{1,0:T(1,128)} %bitcast.6), custom_call_target="tpu_custom_call" | custom-call | tf_op jit(solution)/shard_map/helmholtz/pallas_call | solution.py:368
  152.8 3.6 %copy.7 = f32[17,16,2562]{2,1,0:T(8,128)} copy(f32[17,16,2562]{2,1,0:T(8,128)} %bitcast.5) | data formatting | bytes 5574912

commit v6 on v5

--- a/solution.py
+++ b/solution.py
@@ -145,7 +145,7 @@
         for l in range(levels):
             line = jnp.where(lane < rest, border[pl.ds(l * slots, slots), :], 0.0)
             total = total + (pltpu.roll(line, l * rest, 1) if l else line)
-        edge[...] = total
+        edge[pl.ds(0, slots), :] = total
 
     def gather(c):
         sub = chunks[c][1]
@@ -355,11 +355,11 @@
     largest = max(size + (c == EDGE) for c, (_, size, _) in enumerate(chunks)) * LANES
 
     def buffers(*lead, last=()):
-        shapes = [(*lead, r, LANES) for _, _, r in chunks[:early]]
+        shapes = [(*lead, r, LANES) for _, _, r in chunks[:early] if lead]
         shapes += [(*last, chunks[early][2], LANES)] if last else []
-        return [pltpu.VMEM(shape, jnp.float32) for shape in shapes]
-
-    flat = [pltpu.VMEM((HALVES * number * r, LANES), jnp.float32) for _, _, r in chunks]
+        return [pltpu.VMEM((shape[0] + 1, *shape[1:]), jnp.float32) for shape in shapes]
+
+    flat = [pltpu.VMEM((HALVES * number * r + 128, LANES), jnp.float32) for _, _, r in chunks]
     vmem = pl.BlockSpec(memory_space=pltpu.VMEM)
     smem = pl.BlockSpec(memory_space=pltpu.SMEM)
     hbm = pl.BlockSpec(memory_space=pl.ANY)
@@ -375,15 +375,15 @@
         out_specs=hbm,
         scratch_shapes=[
             pltpu.SMEM((waves,), jnp.int32), pltpu.SMEM((waves,), jnp.int32),
-            [pltpu.VMEM((size, levels * slots, LANES), jnp.float32) for _, size in SPANS],
-            pltpu.VMEM((slots, LANES), jnp.float32),
+            [pltpu.VMEM((size + 1, levels * slots, LANES), jnp.float32) for _, size in SPANS],
+            pltpu.VMEM((slots + 8, LANES), jnp.float32),
             pltpu.VMEM((levels * number, width), jnp.float32),
             pltpu.VMEM((levels * levs, largest), jnp.float32),
             buffers(HALVES * waves, last=(levs, planes)),
             buffers(HALVES * waves, last=(HALVES * waves,)),
             buffers(lines, HALVES * share),
             buffers(lines, HALVES * share, last=(levs, planes)),
-            [*flat[:early], *buffers(last=(levs * planes,))[early:]],
+            [*flat[:early], *buffers(last=(levs * planes,))],
             flat,
             dma((tiles,)), dma,
             dma((early, HALVES * waves)), dma((early, HALVES * waves)),

time: 157 us -> 157 us (level)
  no operation moved by 1% of the time
where the time goes in v6:
time: 157 us; the launch traced here: 156 us
  Pallas kernels  153 us (97%)
  local copies, waits for them, and re-layouts  3.61 us (2%)
    pallas_call x1, Pallas kernels, per_device(): pl.pallas_call(functools.partial(kernel, waves, levs, number, levels, slo...  153 us
    unnamed x1, local copies, waits for them, and re-layouts  3.61 us

profile of v6, /device:TPU:3, one launch (start us, length us, event | category | flops | bytes accessed | tf_op | source)
XLA Modules:
  0.0 156.2 jit_solution(5528578737854155993)
XLA Ops:
  0.0 152.6 %helmholtz.1 = f32[272,2562]{1,0:T(8,128)} custom-call(s32[512]{0:T(512)} %owner.1, f32[544,2562]{1,0:T(8,128)} %bitcast.3, f32[544,2562]{1,0:T(8,128)} %bitcast.4, f32[136,136]{1,0:T(8,128)} %to_modes.1, f32[136,136]{1,0:T(8,128)} %from_modes.1, f32[1,136]{1,0:T(1,128)} %bitcast.6), custom_call_target="tpu_custom_call" | custom-call | tf_op jit(solution)/shard_map/helmholtz/pallas_call | solution.py:368
  152.6 3.6 %copy.7 = f32[17,16,2562]{2,1,0:T(8,128)} copy(f32[17,16,2562]{2,1,0:T(8,128)} %bitcast.5) | data formatting | bytes 5574912
